TPU v7x, 32 devices: a whole 2x2x4 slice. The times are simulated.
32 devices in a mesh: group: 2 (over core), dp: 4 (over y, x), mp: 4 (over z).
Axes of the slice: x: 2, y: 2, z: 4, core: 2. Of those that a mesh axis runs over, the one named last changes fastest.
Arguments:
- x_arrive: bfloat16 [16, 256, 1152], P(('group', 'dp')), may hold values from -6 to 6
- cond_first: int32 [8], P(('group', 'dp')), may hold values 0 or 1
- labels: int32 [8], P(('group', 'dp')), may hold values from 0 to 999
- step_ids: int32 [8], P(('group', 'dp')), may hold values from 0 to 999
- guidance: float32 [1], replicated, may hold values from 2 to 6
- time_table: bfloat16 [1000, 1152], P(None, 'mp'), may hold values from -6 to 6
- class_table: bfloat16 [1001, 1152], P(None, 'mp'), may hold values from -6 to 6
- ada_weight: bfloat16 [1152, 6912], P('mp', 'dp'), may hold values from -0.1875 to 0.1875
- final_ada: bfloat16 [1152, 2304], P('mp'), may hold values from -0.1875 to 0.1875
- qkv_weight: bfloat16 [3, 1152, 1152], P(None, 'dp', 'mp'), may hold values from -2 to 2
- proj_weight: bfloat16 [1152, 1152], P('mp', 'dp'), may hold values from -0.1875 to 0.1875
- fc1_weight: bfloat16 [1152, 4608], P('dp', 'mp'), may hold values from -0.1875 to 0.1875
- fc2_weight: bfloat16 [4608, 1152], P('mp', 'dp'), may hold values from -0.09375 to 0.09375
- out_weight: bfloat16 [1152, 16], replicated, may hold values from -0.1875 to 0.1875
Outputs:
- guided: float32 [8, 4096], P(('group', 'dp'), 'mp')
All inputs are finite; a program needn't handle non-finite values. No bound on the sum of `cond_first` on one device may be relied on, other than what follows from the above.
Results may differ from a plain program's by a relative error of at most 0.025.
Values may be sent and summed in bfloat16 or wider, within the bound.
A program may use at most 64 MiB of HBM per device.

v0:
```python
import jax
import jax.numpy as jnp
from jax import lax
from jax.sharding import PartitionSpec as P

HEADS = 16
CLASSES = 1000


def layer_norm(values):
    mean = jnp.mean(values, axis=-1, keepdims=True)
    centred = values - mean
    spread = jnp.mean(centred * centred, axis=-1, keepdims=True)
    return centred * lax.rsqrt(spread + 1e-06)


def on_device(
    x_arrive,
    cond_first,
    labels,
    step_ids,
    guidance,
    time_table,
    class_table,
    ada_weight,
    final_ada,
    qkv_weight,
    proj_weight,
    fc1_weight,
    fc2_weight,
    out_weight,
):
    pair_count = labels.shape[0]
    tokens = x_arrive.shape[1]
    width = x_arrive.shape[2]
    image_count = 2 * pair_count
    row_count = image_count * tokens
    split_rows = x_arrive.reshape(pair_count, 2, tokens, width)
    first = (cond_first == 1)[:, None, None]
    cond_rows = jnp.where(first, split_rows[:, 0], split_rows[:, 1])
    uncond_rows = jnp.where(first, split_rows[:, 1], split_rows[:, 0])
    x_sides = jnp.stack([cond_rows, uncond_rows])
    time_part = jnp.take(time_table, step_ids, axis=0).astype(jnp.float32)
    class_part = jnp.take(class_table, labels, axis=0).astype(jnp.float32)
    null_part = class_table[CLASSES].astype(jnp.float32)[None, :]
    emb_sides = time_part[None] + jnp.stack([class_part, null_part])
    act_sides = jax.nn.silu(emb_sides).astype(jnp.bfloat16)
    images, acts = (
        lax.all_to_all(x_sides, "group", split_axis=0, concat_axis=0, tiled=True),
        lax.all_to_all(act_sides, "group", split_axis=0, concat_axis=0, tiled=True),
    )
    images = images.reshape(image_count, tokens, width)
    acts = acts.reshape(image_count, act_sides.shape[2])
    partial_final = jnp.dot(acts, final_ada, preferred_element_type=jnp.float32)
    every_act = lax.all_gather(acts, "dp", axis=0, tiled=True)
    column_part = jnp.dot(every_act, ada_weight, preferred_element_type=jnp.float32)
    summed, fmods = (
        lax.psum(column_part.astype(jnp.bfloat16), "mp").astype(jnp.float32),
        lax.psum(partial_final.astype(jnp.bfloat16), "mp").astype(jnp.float32),
    )
    mods = lax.all_to_all(
        summed.astype(jnp.bfloat16), "dp", split_axis=0, concat_axis=1, tiled=True
    ).astype(summed.dtype)
    shift_a, scale_a, gate_a, shift_m, scale_m, gate_m = jnp.split(mods, 6, axis=1)
    shift_f, scale_f = jnp.split(fmods, 2, axis=1)
    images_f = images.astype(jnp.float32)
    hidden = (layer_norm(images_f) * (1.0 + scale_a[:, None]) + shift_a[:, None]).astype(
        jnp.bfloat16
    )
    hidden = hidden.reshape(row_count, width)
    quarter = qkv_weight.shape[2]
    head_dim = width // HEADS
    local_heads = quarter // head_dim
    columns = hidden
    qkv = jnp.einsum(
        "rd,kdc->krc",
        columns,
        lax.all_gather(qkv_weight, "dp", axis=1, tiled=True),
        preferred_element_type=jnp.float32,
    ).astype(jnp.bfloat16)
    query = qkv[0].reshape(image_count, tokens, local_heads, head_dim)
    keys = qkv[1].reshape(image_count, tokens, local_heads, head_dim)
    values = qkv[2].reshape(image_count, tokens, local_heads, head_dim)
    scores = jnp.einsum(
        "bqhe,bkhe->bhqk", query, keys, preferred_element_type=jnp.float32
    ) * head_dim ** (-0.5)
    probs = jax.nn.softmax(scores, axis=-1).astype(jnp.bfloat16)
    mixed = jnp.einsum("bhqk,bkhe->bqhe", probs, values, preferred_element_type=jnp.float32).astype(
        jnp.bfloat16
    )
    mixed = mixed.reshape(row_count, quarter)
    attn_part = jnp.dot(
        mixed,
        lax.all_gather(proj_weight, "dp", axis=1, tiled=True),
        preferred_element_type=jnp.float32,
    )
    attn = (
        lax.psum(attn_part.astype(jnp.bfloat16), "mp")
        .astype(jnp.float32)
        .reshape(image_count, tokens, width)
    )
    first_sum = images_f + gate_a[:, None] * attn
    hidden_two = (layer_norm(first_sum) * (1.0 + scale_m[:, None]) + shift_m[:, None]).astype(
        jnp.bfloat16
    )
    hidden_two = hidden_two.reshape(row_count, width)
    ff_quarter = fc1_weight.shape[1]
    columns = hidden_two
    up = jnp.dot(
        columns,
        lax.all_gather(fc1_weight, "dp", axis=0, tiled=True),
        preferred_element_type=jnp.float32,
    )
    gelu_h = (
        jax.nn.gelu(up, approximate=True)
        .astype(jnp.bfloat16)
        .reshape(image_count, tokens, ff_quarter)
    )
    down_full = lax.all_gather(fc2_weight, "dp", axis=1, tiled=True)
    token_share = tokens // lax.axis_size("mp")
    mlp = lax.psum_scatter(
        jnp.einsum("btf,fd->tbd", gelu_h, down_full, preferred_element_type=jnp.float32).astype(
            jnp.bfloat16
        ),
        "mp",
        scatter_dimension=0,
        tiled=True,
    ).astype(jnp.float32)
    token_start = lax.axis_index("mp") * token_share
    own_first = lax.dynamic_slice_in_dim(first_sum, token_start, token_share, 1).transpose(1, 0, 2)
    second_sum = own_first + gate_m[None] * mlp
    fin = (layer_norm(second_sum) * (1.0 + scale_f[None]) + shift_f[None]).astype(jnp.bfloat16)
    noise = jnp.einsum("tbd,do->bto", fin, out_weight, preferred_element_type=jnp.float32)
    noise = noise.reshape(2, pair_count, token_share * out_weight.shape[1])
    noise = lax.all_to_all(noise, "group", split_axis=0, concat_axis=0, tiled=True)
    return noise[1] + guidance[0] * (noise[0] - noise[1])


def solution(mesh):
    placed = (
        P(("group", "dp"), None, None),
        P(("group", "dp")),
        P(("group", "dp")),
        P(("group", "dp")),
        P(),
        P(None, "mp"),
        P(None, "mp"),
        P("mp", "dp"),
        P("mp", None),
        P(None, "dp", "mp"),
        P("mp", "dp"),
        P("dp", "mp"),
        P("mp", "dp"),
        P(),
    )
    return jax.shard_map(
        on_device, mesh=mesh, in_specs=placed, out_specs=P(("group", "dp"), "mp"), check_vma=False
    )
```

profile of v0, /device:TPU:13, one launch (start us, length us, event | category | flops | bytes accessed | tf_op | source)
XLA Modules:
  0.0 279.5 jit_solution(9953320555875405948)
XLA Ops:
  8.0 1.2 fusion.50
  9.2 1.1 convert_reduce_fusion.1
  10.3 0.5 broadcast.243
  10.8 0.7 reduce.7
  11.5 0.7 reshape.339
  12.1 3.9 %all-to-all-start.1 = ((bf16[2,2,144]{2,1,0:T(2,128)(2,1)}), bf16[2,2,144]{2,1,0:T(2,128)(2,1)S(1)}, u32[]{:S(2)}, u32[]{:S(2)}) async-start(bf16[2,2,144]{2,1,0:T(2,128)(2,1)} %reshape.339), calls=%async_computation.1 | async-start | bytes 4096 | tf_op jit(solution)/shard_map/all_to_all | solution.py:50
  16.1 2.5 copy.61
  18.5 0.0 all-gather.5.cloned.1.call-update
  19.2 0.1 broadcast_select_fusion.1
  19.3 0.0 copy-start.4
  19.3 1.1 pad_maximum_fusion
  20.5 0.0 all-to-all-done.1
  20.5 3.7 %all-to-all-start = ((bf16[2,1,256,1152]{3,2,1,0:T(8,128)(2,1)}), bf16[2,1,256,1152]{3,2,1,0:T(8,128)(2,1)S(1)}, u32[]{:S(2)}, u32[]{:S(2)}) async-start(bf16[2,1,256,1152]{3,2,1,0:T(8,128)(2,1)} %pad_maximum_fusion), calls=%async_computation | async-start | bytes 2359296 | tf_op jit(solution)/shard_map/all_to_all | solution.py:49
  24.1 0.1 reshape.340
  24.2 6.4 %all-gather = bf16[8,1,288]{2,1,0:T(2,128)(2,1)S(1)} all-gather(bf16[2,1,288]{2,1,0:T(2,128)(2,1)S(1)} %reshape.340), channel_id=2, replica_groups=mesh['group'=2,'dp'=4,'mp'=4] {'dp'}, dimensions={0}, use_global_device_ids=true | all-gather | bytes 5760 | tf_op jit(solution)/shard_map/all_gather | solution.py:55
  30.7 0.9 convolution_convert_fusion.3
  31.5 0.8 all_to_all.21
  32.3 1.8 copy.68
  34.1 0.3 convolution_convert_fusion
  34.4 13.5 %all-reduce = (bf16[2,2304]{1,0:T(2,128)(2,1)S(1)}, bf16[4,2,1728]{2,1,0:T(2,128)(2,1)}) all-reduce(bf16[2,2304]{1,0:T(2,128)(2,1)S(1)} %convolution_convert_fusion, bf16[4,2,1728]{2,1,0:T(2,128)(2,1)S(1)} %all_to_all.21), channel_id=1, replica_groups=mesh['group'=2,'dp'=4,'mp'=4] {'mp'}, use_global_device_ids=true, to_apply=%region_11.12 | all-reduce | flops 18432 | bytes 73728 | tf_op jit(solution)/shard_map/psum | solution.py:59
  47.9 0.0 all-to-all-done
  47.9 3.3 %all-to-all-start.2 = ((bf16[4,2,1728]{2,1,0:T(2,128)(2,1)}), bf16[4,2,1728]{2,1,0:T(2,128)(2,1)S(1)}, u32[]{:S(2)}, u32[]{:S(2)}) async-start(bf16[4,2,1728]{2,1,0:T(2,128)(2,1)} %get-tuple-element.30), calls=%async_computation.2 | async-start | bytes 57344 | tf_op jit(solution)/shard_map/all_to_all | solution.py:61
  51.1 0.0 all-reduce.3.cloned.1.call-start
  51.2 0.2 convert_reduce_fusion
  51.4 0.5 fusion.21
  51.9 0.2 copy-done.5
  52.1 18.8 %all_gather.17 = bf16[288,1152]{0,1:T(8,128)(2,1)S(1)} all-gather(bf16[288,288]{0,1:T(8,128)(2,1)S(1)} %copy-done.5), channel_id=1, replica_groups=mesh['group'=2,'dp'=4,'mp'=4] {'dp'}, dimensions={1}, use_global_device_ids=true | all-gather | bytes 829440 | tf_op jit(solution)/shard_map/all_gather | solution.py:94
  70.9 0.0 all-to-all-done.2
  71.0 0.1 reshape.315
  71.1 1.7 fusion.17
  72.8 3.7 %fusion.27 = bf16[3,512,288]{1,2,0:T(8,128)(2,1)S(1)} fusion(bf16[3,1152,288]{2,0,1:T(4,128)(2,1)} %all-gather.5.cloned.1.call-done, bf16[512,1152]{1,0:T(8,128)(2,1)} %fusion.17), kind=kOutput, calls=%fused_computation.42 | convolution fusion | flops 1019658240 | bytes 4055040 | tf_op jit(solution)/shard_map/rd,kdc->krc/dot_general | solution.py:75
  76.6 1.0 fusion.70
  77.5 1.8 reshape_squeeze.10
  79.3 1.7 reshape_squeeze.11
  81.1 1.7 reshape_squeeze.9
  82.8 3.2 %fusion.72 = (f32[2,4,256]{2,1,0:T(4,128)S(1)}, f32[2,4,256,256]{2,3,1,0:T(8,128)}) fusion(bf16[2,256,4,72]{1,0,3,2:T(2,128)(2,1)} %reshape_squeeze.11, bf16[2,256,4,72]{1,0,3,2:T(2,128)(2,1)} %reshape_squeeze.10), kind=kOutput, calls=%fused_computation.99 | convolution fusion | flops 77070592 | bytes 2695168 | tf_op jit(solution)/shard_map/sub | solution.py:87
  86.0 2.0 fusion.31
  88.1 0.3 copy.67
  88.4 1.9 convolution_convert_fusion.2
  90.3 0.0 all-reduce.3.cloned.1.call-update
  90.4 0.0 all-gather.7.cloned.1.call-start
  90.4 0.7 all-gather.7.cloned.1.call-update
  91.1 0.0 all-gather.9.cloned.1.call-start
  91.1 0.5 all-gather.9.cloned.1.call-update
  91.7 0.2 reduce-scatter.2.cloned.1.call-start
  91.9 56.6 %all-reduce.3.cloned.1.call-done = bf16[512,1152]{1,0:T(8,128)(2,1)} async-done(((bf16[512,1152]{1,0:T(8,128)(2,1)}), bf16[512,1152]{1,0:T(8,128)(2,1)}) %all-reduce.3.cloned.1.call-update) | async-done | bytes 1179664 | tf_op jit(solution)/shard_map/psum | solution.py:98
  148.5 1.7 fusion.68
  150.3 1.4 copy-done.1
  151.7 0.4 multiply_reduce_fusion
  152.1 0.3 copy-done.2
  152.4 2.0 fusion.13
  154.4 35.6 %all-gather.7.cloned.1.call-done = bf16[1152,1152]{1,0:T(8,128)(2,1)} async-done(((bf16[288,1152]{1,0:T(8,128)(2,1)}), bf16[1152,1152]{1,0:T(8,128)(2,1)}) %all-gather.7.cloned.1.call-update) | async-done | bytes 2654224 | tf_op jit(solution)/shard_map/all_gather | solution.py:111
  190.0 4.0 %fusion.12 = bf16[512,1152]{1,0:T(8,128)(2,1)S(1)} fusion(bf16[512,1152]{1,0:T(8,128)(2,1)} %fusion.13, bf16[1152,1152]{1,0:T(8,128)(2,1)} %all-gather.7.cloned.1.call-done), kind=kOutput, calls=%fused_computation.16 | convolution fusion | flops 1364262912 | bytes 5013504 | tf_op jit(solution)/shard_map/dot_general | solution.py:109
  194.0 37.5 %all-gather.9.cloned.1.call-done = bf16[1152,1152]{0,1:T(8,128)(2,1)} async-done(((bf16[1152,288]{0,1:T(8,128)(2,1)}), bf16[1152,1152]{0,1:T(8,128)(2,1)}) %all-gather.9.cloned.1.call-update) | async-done | bytes 2654224 | tf_op jit(solution)/shard_map/all_gather | solution.py:119
  231.5 4.6 %fusion.1 = bf16[256,2,1152]{2,0,1:T(8,128)(2,1)} fusion(bf16[2,256,1152]{2,1,0:T(8,128)(2,1)S(1)} %bitcast.150, bf16[1152,1152]{0,1:T(8,128)(2,1)} %all-gather.9.cloned.1.call-done), kind=kOutput, calls=%fused_computation.5 | convolution fusion | flops 1359544320 | bytes 5013504 | tf_op jit(solution)/shard_map/btf,fd->tbd/dot_general | solution.py:122
  236.2 0.0 reduce-scatter.2.cloned.1.call-update
  236.9 26.7 %reduce-scatter.2.cloned.1.call-done = bf16[64,2,1152]{2,0,1:T(8,128)(2,1)} async-done(((bf16[256,2,1152]{2,0,1:T(8,128)(2,1)}), bf16[64,2,1152]{2,0,1:T(8,128)(2,1)}) %reduce-scatter.2.cloned.1.call-update) | async-done | bytes 294928 | tf_op jit(solution)/shard_map/reduce_scatter | solution.py:121
  263.6 1.3 fusion.49
  264.9 1.4 multiply_reduce_fusion.2
  266.3 1.4 convolution_bitcast_fusion
  267.7 0.1 copy.69
  267.8 0.2 reshape.335
  268.0 4.3 %all_to_all.28 = f32[2,1,1024]{2,1,0:T(1,128)S(1)} all-to-all(f32[2,1,1024]{2,1,0:T(1,128)S(1)} %reshape.335), channel_id=1, replica_groups=mesh['group'=2,'dp'=4,'mp'=4] {'group'}, dimensions={0} | all-to-all | bytes 16384 | tf_op jit(solution)/shard_map/all_to_all | solution.py:135
  272.4 0.6 fusion.56
  (31 shorter events, 0.2 us)
Async XLA Ops:
  6.5 27.5 %copy-start = (bf16[288,2304]{1,0:T(8,128)(2,1)S(1)}, bf16[288,2304]{1,0:T(8,128)(2,1)}, u32[]{:S(2)}) copy-start(bf16[288,2304]{1,0:T(8,128)(2,1)} %param.22) | copy-start | bytes 3981316
  6.5 12.7 %copy-start.3 = (bf16[2,256,1152]{2,1,0:T(8,128)(2,1)S(1)}, bf16[2,256,1152]{2,1,0:T(8,128)(2,1)}, u32[]{:S(2)}) copy-start(bf16[2,256,1152]{2,1,0:T(8,128)(2,1)} %param.14) | copy-start | bytes 3538948
  12.1 8.3 %all-to-all-start.1 = ((bf16[2,2,144]{2,1,0:T(2,128)(2,1)}), bf16[2,2,144]{2,1,0:T(2,128)(2,1)S(1)}, u32[]{:S(2)}, u32[]{:S(2)}) async-start(bf16[2,2,144]{2,1,0:T(2,128)(2,1)} %reshape.339), calls=%async_computation.1 | async-start | bytes 4096 | tf_op jit(solution)/shard_map/all_to_all | solution.py:50
  16.1 56.8 %all-gather.5.cloned.1.call-start = ((), (), s32[]{:S(2)}) async-start(), calls=%async_computation.5 | async-start | bytes 4423680 | tf_op jit(solution)/shard_map/all_gather | solution.py:78
  19.3 11.3 %copy-start.4 = (bf16[288,1728]{1,0:T(8,128)(2,1)S(1)}, bf16[288,1728]{1,0:T(8,128)(2,1)}, u32[]{:S(2)}) copy-start(bf16[288,1728]{1,0:T(8,128)(2,1)} %param.21) | copy-start | bytes 2985988
  20.5 27.4 %all-to-all-start = ((bf16[2,1,256,1152]{3,2,1,0:T(8,128)(2,1)}), bf16[2,1,256,1152]{3,2,1,0:T(8,128)(2,1)S(1)}, u32[]{:S(2)}, u32[]{:S(2)}) async-start(bf16[2,1,256,1152]{3,2,1,0:T(8,128)(2,1)} %pad_maximum_fusion), calls=%async_computation | async-start | bytes 2359296 | tf_op jit(solution)/shard_map/all_to_all | solution.py:49
  47.9 23.1 %all-to-all-start.2 = ((bf16[4,2,1728]{2,1,0:T(2,128)(2,1)}), bf16[4,2,1728]{2,1,0:T(2,128)(2,1)S(1)}, u32[]{:S(2)}, u32[]{:S(2)}) async-start(bf16[4,2,1728]{2,1,0:T(2,128)(2,1)} %get-tuple-element.30), calls=%async_computation.2 | async-start | bytes 57344 | tf_op jit(solution)/shard_map/all_to_all | solution.py:61
  51.1 97.4 %all-reduce.3.cloned.1.call-start = ((), (), s32[]{:S(2)}) async-start(), calls=%async_computation.6 | async-start | bytes 2359296 | tf_op jit(solution)/shard_map/psum | solution.py:98
  51.2 0.9 copy-start.5
  90.4 99.7 %all-gather.7.cloned.1.call-start = ((), (), s32[]{:S(2)}) async-start(), calls=%async_computation.7 | async-start | bytes 3317760 | tf_op jit(solution)/shard_map/all_gather | solution.py:111
  91.1 140.4 %all-gather.9.cloned.1.call-start = ((), (), s32[]{:S(2)}) async-start(), calls=%async_computation.8 | async-start | bytes 3317760 | tf_op jit(solution)/shard_map/all_gather | solution.py:119
  91.7 171.9 %reduce-scatter.2.cloned.1.call-start = ((), (), s32[]{:S(2)}) async-start(), calls=%async_computation.9 | async-start | bytes 1474560 | tf_op jit(solution)/shard_map/reduce_scatter | solution.py:121
  150.3 1.5 copy-start.1
  150.3 2.1 copy-start.2
  236.2 30.1 %copy-start.6 = (bf16[1152,16]{0,1:T(8,128)(2,1)S(1)}, bf16[1152,16]{0,1:T(8,128)(2,1)}, u32[]{:S(2)}) copy-start(bf16[1152,16]{0,1:T(8,128)(2,1)} %param.27) | copy-start | bytes 110596
Sparse Core Ops, SparseCore 0:
  18.7 53.0 all-gather.4
  90.5 58.0 all-reduce.2
  150.4 39.6 all-gather.6
  191.7 39.7 all-gather.8
  236.3 27.2 reduce-scatter.1
where the time goes:
time: 284 us; the launch traced here: 279 us
  waiting for transfers between devices  158 us (56%)
  blocking collectives  43.1 us (15%)
  matrix products  22.2 us (8%)
  between operations  16.1 us (6%)
  local copies, waits for them, and re-layouts  15.2 us (5%)
  other arithmetic  14 us (5%)
  starting transfers between devices  11.2 us (4%)
    psum x1, waiting for transfers between devices, on_device(): lax.psum(attn_part.astype(jnp.bfloat16), 'mp').astype(jnp.float32)  56.6 us
    all_gather x1, waiting for transfers between devices, on_device(): down_full = lax.all_gather(fc2_weight, 'dp', axis=1, tiled=True)  37.5 us
    all_gather x1, waiting for transfers between devices, on_device(): lax.all_gather(fc1_weight, 'dp', axis=0, tiled=True)  35.6 us
    reduce_scatter x1, waiting for transfers between devices, on_device(): lax.psum_scatter(jnp.einsum('btf,fd->tbd', gelu_h, down_full, preferred_e...  26.7 us
    all_gather x1, blocking collectives, on_device(): lax.all_gather(proj_weight, 'dp', axis=1, tiled=True)  18.8 us
    psum x1, blocking collectives, on_device(): lax.psum(partial_final.astype(jnp.bfloat16), 'mp').astype(jnp.float32)  13.5 us
    unnamed x23, local copies, waits for them, and re-layouts  7.01 us
    all_gather x1, blocking collectives, on_device(): every_act = lax.all_gather(acts, 'dp', axis=0, tiled=True)  6.45 us
  transfers between devices with their start and end apart: 8, of which 4 were waited for; matrix products, arithmetic and copies ran while one was open for 6% of the time, Pallas kernels for 0%

commit v1 on v0

--- a/solution.py
+++ b/solution.py
@@ -1,7 +1,10 @@
 import jax
 import jax.numpy as jnp
 from jax import lax
+from jax.experimental import pallas as pl
+from jax.experimental.pallas import tpu as pltpu
 from jax.sharding import PartitionSpec as P
+import functools
 
 HEADS = 16
 CLASSES = 1000
@@ -136,6 +139,397 @@
     return noise[1] + guidance[0] * (noise[0] - noise[1])
 
 
+MESH = pl.DeviceIdType.MESH
+BF = jnp.bfloat16
+F32 = jnp.float32
+
+
+def dot_nt(a, b):
+    return lax.dot_general(a, b, (((1,), (1,)), ((), ())), preferred_element_type=F32)
+
+
+class Copies:
+    def __init__(self, send, recv):
+        self.send, self.recv, self.count, self.sent = send, recv, 0, []
+
+    def slots(self, number):
+        first = self.count
+        self.count += number
+        return first
+
+    def make(self, src, dst, k, dev):
+        return pltpu.make_async_remote_copy(
+            src_ref=src,
+            dst_ref=dst,
+            send_sem=self.send.at[k],
+            recv_sem=self.recv.at[k],
+            device_id=dev,
+            device_id_type=MESH,
+        )
+
+    def start(self, src, dst, k, dev):
+        copy = self.make(src, dst, k, dev)
+        copy.start()
+        self.sent.append(copy)
+
+    def arrived(self, dst, k, dev):
+        self.make(dst, dst, k, dev).wait_recv()
+
+    def drain(self):
+        for copy in self.sent:
+            copy.wait_send()
+        self.sent = []
+
+
+def copy_count(nd, nm):
+    per_weight = 2 * (nd - 1)
+    return (
+        (nd - 1)
+        + (nd * nm - 1)
+        + (nm - 1)
+        + 3 * per_weight
+        + 2 * (nm - 1)
+        + per_weight
+        + 2 * (nm - 1)
+        + (nm - 1)
+    )
+
+
+def block_kernel(
+    nd,
+    nm,
+    head_dim,
+    x_ref,
+    act_ref,
+    ada_ref,
+    fada_ref,
+    qkv_ref,
+    proj_ref,
+    fc1_ref,
+    fc2_ref,
+    outw_ref,
+    eps_ref,
+    act_all,
+    mod_part,
+    mod_all,
+    fmod_part,
+    fmod_all,
+    qkv_all,
+    proj_all,
+    fc1_all,
+    fc2_all,
+    h_ref,
+    q_ref,
+    mix_all,
+    x1_ref,
+    gelu_ref,
+    rs_send,
+    rs_recv,
+    send_sem,
+    recv_sem,
+):
+    g, d, m = lax.axis_index("group"), lax.axis_index("dp"), lax.axis_index("mp")
+    images, tokens, width = x_ref.shape
+    sib = {"group": 1 - g}
+
+    def dpp(k):
+        return lax.rem(d + k + nd, nd)
+
+    def mpp(k):
+        return lax.rem(m + k + nm, nm)
+
+    barrier = pltpu.get_barrier_semaphore()
+    for a in range(nd):
+        for b in range(nm):
+            if a or b:
+                pl.semaphore_signal(
+                    barrier, inc=1, device_id={"dp": dpp(a), "mp": mpp(b)}, device_id_type=MESH
+                )
+    pl.semaphore_signal(barrier, inc=1, device_id=sib, device_id_type=MESH)
+    pl.semaphore_wait(barrier, nd * nm)
+
+    cp = Copies(send_sem, recv_sem)
+
+    k_act = cp.slots(nd - 1)
+    for a in range(1, nd):
+        cp.start(act_ref, act_all.at[d], k_act + a - 1, {"dp": dpp(a)})
+    k_pz = cp.slots(nm - 1)
+    for b in range(1, nm):
+        cp.start(proj_ref.at[g], proj_all.at[m, d, g], k_pz + b - 1, {"mp": mpp(b)})
+
+    def gather_start(src, buf):
+        k = cp.slots(nd - 1)
+        for a in range(1, nd):
+            cp.start(src.at[g], buf.at[d, g], k + a - 1, {"dp": dpp(a)})
+        return k
+
+    def gather_forward(buf, k):
+        kf = cp.slots(nd - 1)
+        for a in range(1, nd):
+            cp.arrived(buf.at[dpp(-a), g], k + a - 1, {"dp": dpp(-a)})
+            cp.start(buf.at[dpp(-a), g], buf.at[dpp(-a), g], kf + a - 1, sib)
+        return kf
+
+    def gather_finish(buf, kf):
+        for a in range(1, nd):
+            cp.arrived(buf.at[dpp(-a), 1 - g], kf + a - 1, sib)
+
+    k_qkv = gather_start(qkv_ref, qkv_all)
+    act_all[pl.ds(d, 1)] = act_ref[...][None]
+    qkv_all[pl.ds(d, 1)] = qkv_ref[...][None]
+    proj_all[pl.ds(m, 1), pl.ds(d, 1)] = proj_ref[...][None, None]
+    fc1_all[pl.ds(d, 1)] = fc1_ref[...][None]
+    fc2_all[pl.ds(d, 1)] = fc2_ref[...][None]
+
+    pad = act_ref.shape[0]
+    fpart = jnp.dot(act_ref[...].astype(BF), fada_ref[...], preferred_element_type=F32)
+    fmod_part[...] = fpart[:images]
+    fmod_all[pl.ds(m, 1)] = fpart[:images][None]
+    for a in range(1, nd):
+        cp.arrived(act_all.at[dpp(-a)], k_act + a - 1, {"dp": dpp(-a)})
+    acts = act_all[...].reshape(nd * pad, act_ref.shape[1]).astype(BF)
+    part = jnp.dot(acts, ada_ref[...], preferred_element_type=F32)
+    for a in range(nd):
+        mod_part[a] = part[a * pad : a * pad + images]
+    mod_all[pl.ds(d, 1), pl.ds(m, 1)] = mod_part[pl.ds(d, 1)][None]
+    k_mod = cp.slots(nd * nm - 1)
+    for a in range(nd):
+        for b in range(nm):
+            if a or b:
+                cp.start(
+                    mod_part.at[dpp(a)],
+                    mod_all.at[d, m],
+                    k_mod + a * nm + b - 1,
+                    {"dp": dpp(a), "mp": mpp(b)},
+                )
+    k_fmod = cp.slots(nm - 1)
+    for b in range(1, nm):
+        cp.start(fmod_part, fmod_all.at[m], k_fmod + b - 1, {"mp": mpp(b)})
+
+    for b in range(1, nm):
+        cp.arrived(proj_all.at[mpp(-b), d, g], k_pz + b - 1, {"mp": mpp(-b)})
+    k_pd = cp.slots(nd - 1)
+    for a in range(1, nd):
+        cp.start(proj_all.at[:, d, g], proj_all.at[:, d, g], k_pd + a - 1, {"dp": dpp(a)})
+    k_fc1 = gather_start(fc1_ref, fc1_all)
+    k_fc2 = gather_start(fc2_ref, fc2_all)
+    f_qkv = gather_forward(qkv_all, k_qkv)
+    k_pzs = cp.slots(nm - 1)
+    for b in range(1, nm):
+        cp.start(
+            proj_all.at[mpp(-b), d, g], proj_all.at[mpp(-b), d, g], k_pzs + b - 1, sib
+        )
+
+    for a in range(nd):
+        for b in range(nm):
+            if a or b:
+                cp.arrived(
+                    mod_all.at[dpp(-a), mpp(-b)],
+                    k_mod + a * nm + b - 1,
+                    {"dp": dpp(-a), "mp": mpp(-b)},
+                )
+    mods = jnp.concatenate(
+        [functools.reduce(jnp.add, [mod_all[a, b] for b in range(nm)]) for a in range(nd)], axis=1
+    )
+
+    def piece(k, i):
+        return mods[i : i + 1, k * width : (k + 1) * width]
+
+    step = tokens // 4
+
+    for i in range(images):
+        shift, scale = piece(0, i), piece(1, i)
+
+        @pl.loop(0, 4)
+        def _(c):
+            rows = pl.ds(pl.multiple_of(c * step, step), step)
+            v = x_ref[i, rows, :].astype(F32)
+            h_ref[i, rows, :] = (layer_norm(v) * (1.0 + scale) + shift).astype(BF)
+
+    gather_finish(qkv_all, f_qkv)
+    quarter = qkv_ref.shape[3]
+    heads = quarter // head_dim
+    lane = lax.broadcasted_iota(jnp.int32, (1, quarter), 1)
+    k_mix = cp.slots(images * (nm - 1))
+    for i in range(images):
+        for j in range(3):
+            w = qkv_all[:, :, j].reshape(width, quarter)
+            q_ref[j] = jnp.dot(h_ref[i], w, preferred_element_type=F32).astype(BF)
+        total = jnp.zeros((tokens, quarter), F32)
+        for n in range(heads):
+            own = (lane >= n * head_dim) & (lane < (n + 1) * head_dim)
+            own = jnp.where(own, 1.0, 0.0).astype(BF)
+            s = dot_nt(q_ref[0] * own, q_ref[1]) * head_dim ** (-0.5)
+            e = jnp.exp(s - jnp.max(s, axis=-1, keepdims=True))
+            p = (e / jnp.sum(e, axis=-1, keepdims=True)).astype(BF)
+            total = total + jnp.dot(p, q_ref[2] * own, preferred_element_type=F32)
+        mix_all[pl.ds(m, 1), i] = total.astype(BF)[None]
+        for b in range(1, nm):
+            cp.start(
+                mix_all.at[m, i],
+                mix_all.at[m, i],
+                k_mix + i * (nm - 1) + b - 1,
+                {"mp": mpp(b)},
+            )
+
+    k_pds = cp.slots(nd - 1)
+    for a in range(1, nd):
+        cp.arrived(proj_all.at[:, dpp(-a), g], k_pd + a - 1, {"dp": dpp(-a)})
+        cp.start(
+            proj_all.at[:, dpp(-a), g], proj_all.at[:, dpp(-a), g], k_pds + a - 1, sib
+        )
+    for b in range(1, nm):
+        cp.arrived(proj_all.at[mpp(-b), d, 1 - g], k_pzs + b - 1, sib)
+    f_fc1 = gather_forward(fc1_all, k_fc1)
+    for a in range(1, nd):
+        cp.arrived(proj_all.at[:, dpp(-a), 1 - g], k_pds + a - 1, sib)
+
+    for i in range(images):
+        for b in range(1, nm):
+            cp.arrived(
+                mix_all.at[mpp(-b), i], k_mix + i * (nm - 1) + b - 1, {"mp": mpp(-b)}
+            )
+        gate, shift, scale = piece(2, i), piece(3, i), piece(4, i)
+
+        @pl.loop(0, 2)
+        def _(c):
+            rows = pl.ds(pl.multiple_of(c * 2 * step, 2 * step), 2 * step)
+            attn = jnp.zeros((2 * step, width), F32)
+            for b in range(nm):
+                attn = attn + dot_nt(mix_all[b, i, rows, :], proj_all[b].reshape(width, quarter))
+            v = x_ref[i, rows, :].astype(F32) + gate * attn
+            x1_ref[i, rows, :] = v
+            h_ref[i, rows, :] = (layer_norm(v) * (1.0 + scale) + shift).astype(BF)
+
+    gather_finish(fc1_all, f_fc1)
+    ff = fc1_ref.shape[2]
+    for i in range(images):
+
+        @pl.loop(0, 2)
+        def _(c):
+            rows = pl.ds(pl.multiple_of(c * 2 * step, 2 * step), 2 * step)
+            up = jnp.dot(
+                h_ref[i, rows, :], fc1_all[...].reshape(width, ff), preferred_element_type=F32
+            )
+            gelu_ref[i, rows, :] = jax.nn.gelu(up, approximate=True).astype(BF)
+
+    f_fc2 = gather_forward(fc2_all, k_fc2)
+    gather_finish(fc2_all, f_fc2)
+
+    share = tokens // nm
+    k_rs = cp.slots(nm - 1)
+    own_rows = pl.ds(pl.multiple_of(m * share, share), share)
+
+    def down(rows):
+        left = gelu_ref[:, rows, :].reshape(images * share, ff)
+        return dot_nt(left, fc2_all[...].reshape(width, ff))
+
+    for b in range(1, nm):
+        rows = pl.ds(pl.multiple_of(mpp(b) * share, share), share)
+        rs_send[b - 1] = down(rows).astype(BF)
+        cp.start(rs_send.at[b - 1], rs_recv.at[b - 1], k_rs + b - 1, {"mp": mpp(b)})
+    mlp = down(own_rows)
+    for b in range(1, nm):
+        cp.arrived(fmod_all.at[mpp(-b)], k_fmod + b - 1, {"mp": mpp(-b)})
+    fmods = functools.reduce(jnp.add, [fmod_all[b] for b in range(nm)])
+    for b in range(1, nm):
+        cp.arrived(rs_recv.at[b - 1], k_rs + b - 1, {"mp": mpp(-b)})
+        mlp = mlp + rs_recv[b - 1].astype(F32)
+    for i in range(images):
+        v = x1_ref[i, own_rows, :] + piece(5, i) * mlp[i * share : (i + 1) * share]
+        shift, scale = fmods[i : i + 1, :width], fmods[i : i + 1, width:]
+        fin = (layer_norm(v) * (1.0 + scale) + shift).astype(BF)
+        eps_ref[i] = jnp.dot(fin, outw_ref[...], preferred_element_type=F32)
+    cp.drain()
+
+
+def on_device_kernel(
+    x_arrive,
+    cond_first,
+    labels,
+    step_ids,
+    guidance,
+    time_table,
+    class_table,
+    ada_weight,
+    final_ada,
+    qkv_weight,
+    proj_weight,
+    fc1_weight,
+    fc2_weight,
+    out_weight,
+):
+    nd, nm = lax.axis_size("dp"), lax.axis_size("mp")
+    images, tokens, width = x_arrive.shape
+    rows, quarter = qkv_weight.shape[1:]
+    half = rows // 2
+    ff = fc1_weight.shape[1]
+    time_part = lax.dynamic_slice_in_dim(time_table, step_ids[0], 1, 0).astype(F32)
+    class_part = lax.dynamic_slice_in_dim(class_table, labels[0], 1, 0).astype(F32)
+    null_part = class_table[CLASSES].astype(F32)[None, :]
+    first = cond_first[0] == 1
+    act = jax.nn.silu(
+        time_part
+        + jnp.concatenate(
+            [
+                jnp.where(first, class_part, null_part),
+                jnp.where(first, null_part, class_part),
+            ]
+        )
+    ).astype(BF)
+    act = jnp.pad(act.astype(F32), ((0, 8 - images), (0, 0)))
+    qkv_in = qkv_weight.reshape(3, 2, half, quarter).transpose(1, 0, 2, 3)
+    proj_in = proj_weight.T.reshape(2, half, quarter)
+    fc1_in = fc1_weight.reshape(2, half, ff)
+    fc2_in = fc2_weight.T.reshape(2, half, ff)
+    copies = copy_count(nd, nm)
+    vmem = pl.BlockSpec(memory_space=pltpu.VMEM)
+    share = tokens // nm
+    eps = pl.pallas_call(
+        functools.partial(block_kernel, nd, nm, width // HEADS),
+        out_shape=jax.ShapeDtypeStruct((images, share, out_weight.shape[1]), F32),
+        in_specs=[vmem] * 9,
+        out_specs=vmem,
+        scratch_shapes=[
+            pltpu.VMEM((nd,) + act.shape, F32),
+            pltpu.VMEM((nd, images, ada_weight.shape[1]), F32),
+            pltpu.VMEM((nd, nm, images, ada_weight.shape[1]), F32),
+            pltpu.VMEM((images, final_ada.shape[1]), F32),
+            pltpu.VMEM((nm, images, final_ada.shape[1]), F32),
+            pltpu.VMEM((nd, 2, 3, half, quarter), BF),
+            pltpu.VMEM((nm, nd, 2, half, quarter), BF),
+            pltpu.VMEM((nd, 2, half, ff), BF),
+            pltpu.VMEM((nd, 2, half, ff), BF),
+            pltpu.VMEM((images, tokens, width), BF),
+            pltpu.VMEM((3, tokens, quarter), BF),
+            pltpu.VMEM((nm, images, tokens, quarter), BF),
+            pltpu.VMEM((images, tokens, width), F32),
+            pltpu.VMEM((images, tokens, ff), BF),
+            pltpu.VMEM((nm - 1, images * share, width), BF),
+            pltpu.VMEM((nm - 1, images * share, width), BF),
+            pltpu.SemaphoreType.DMA((copies,)),
+            pltpu.SemaphoreType.DMA((copies,)),
+        ],
+        compiler_params=pltpu.CompilerParams(
+            collective_id=0, has_side_effects=True, vmem_limit_bytes=60 * 1024 * 1024
+        ),
+        name="dit_block",
+    )(
+        x_arrive,
+        act,
+        ada_weight,
+        final_ada,
+        qkv_in,
+        proj_in,
+        fc1_in,
+        fc2_in,
+        out_weight,
+    )
+    cond = jnp.where(first, eps[0], eps[1])
+    uncond = jnp.where(first, eps[1], eps[0])
+    return (uncond + guidance[0] * (cond - uncond)).reshape(1, share * out_weight.shape[1])
+
+
 def solution(mesh):
     placed = (
         P(("group", "dp"), None, None),
@@ -153,6 +547,11 @@
         P("mp", "dp"),
         P(),
     )
+    def body(*args):
+        rows = args[9].shape[1]
+        fits = args[0].shape[0] == 2 and mesh.shape["group"] == 2 and rows % 32 == 0
+        return on_device_kernel(*args) if fits else on_device(*args)
+
     return jax.shard_map(
-        on_device, mesh=mesh, in_specs=placed, out_specs=P(("group", "dp"), "mp"), check_vma=False
-    )
+        body, mesh=mesh, in_specs=placed, out_specs=P(("group", "dp"), "mp"), check_vma=False
+    )

time: 284 us -> 117 us (0.41); the launches traced: 279 us -> 116 us
  waiting for transfers between devices: 158 us -> 0 us
  Pallas kernels: 0 us -> 105 us
  blocking collectives: 43.1 us -> 0 us
  matrix products: 22.2 us -> 0 us
  between operations: 16.1 us -> 2.72 us
  starting transfers between devices: 11.2 us -> 0 us
  other arithmetic: 14 us -> 3.1 us
  local copies, waits for them, and re-layouts: 15.2 us -> 5.18 us
    pallas_call x0 -> x1, Pallas kernels: none -> 105 us  [on_device_kernel(): pl.pallas_call(functools.partial(block_kernel, nd, nm, width // HEADS), o...]
    all_gather x3 -> x0, waiting for transfers between devices: 73.1 us -> none  [the longest x1 37.5 us: on_device(): down_full = lax.all_gather(fc2_weight, 'dp', axis=1, tiled=True)]
    psum x1 -> x0, waiting for transfers between devices: 56.6 us -> none  [on_device(): lax.psum(attn_part.astype(jnp.bfloat16), 'mp').astype(jnp.float32)]
    reduce_scatter x1 -> x0, waiting for transfers between devices: 26.7 us -> none  [on_device(): lax.psum_scatter(jnp.einsum('btf,fd->tbd', gelu_h, down_full, preferred_e...]
    all_gather x2 -> x0, blocking collectives: 25.3 us -> none  [the longest x1 18.8 us: on_device(): lax.all_gather(proj_weight, 'dp', axis=1, tiled=True)]
    dot_general x8 -> x0, matrix products: 18.9 us -> none  [the longest x1 4.65 us: on_device(): jnp.einsum('btf,fd->tbd', gelu_h, down_full, preferred_element_type=jnp.f...]
    psum x1 -> x0, blocking collectives: 13.5 us -> none  [on_device(): lax.psum(partial_final.astype(jnp.bfloat16), 'mp').astype(jnp.float32)]
    all_to_all x3 -> x0, starting transfers between devices: 10.8 us -> none  [the longest x1 3.92 us: on_device(): lax.all_to_all(act_sides, 'group', split_axis=0, concat_axis=0, tiled=True)]
  transfers between devices with their start and end apart: 8 -> 0, of which waited for: 4 -> 0; matrix products, arithmetic and copies ran while one was open for 6% -> 0% of each run, Pallas kernels for 0% -> 0%
where the time goes in v1:
time: 117 us; the launch traced here: 116 us
  Pallas kernels  105 us (90%)
  local copies, waits for them, and re-layouts  5.18 us (4%)
  other arithmetic  3.1 us (3%)
  between operations  2.72 us (2%)
    pallas_call x1, Pallas kernels, on_device_kernel(): pl.pallas_call(functools.partial(block_kernel, nd, nm, width // HEADS), o...  105 us

profile of v1, /device:TPU:13, one launch (start us, length us, event | category | flops | bytes accessed | tf_op | source)
XLA Modules:
  0.0 116.2 jit_solution(13847051015078771018)
XLA Ops:
  0.0 0.0 copy-start.1
  0.0 0.0 copy-start
  0.7 1.1 constant_dynamic-slice_fusion
  1.8 0.1 copy.24
  1.9 0.1 copy.25
  3.3 1.1 convert_reduce_fusion
  4.4 0.6 pad_convert_fusion.act_ref
  5.0 2.0 %copy.27 = bf16[3,2,144,288]{3,2,0,1:T(8,128)(2,1)} copy(bf16[3,2,144,288]{3,2,1,0:T(8,128)(2,1)} %bitcast.23) | data formatting | bytes 995328 | tf_op jit(solution)/shard_map/reshape | solution.py:481
  7.0 0.0 copy-done.1
  7.0 0.9 copy.23.outw_ref
  7.9 0.0 copy-done
  7.9 0.8 copy.22
  8.8 105.2 %dit_block.1 = f32[2,64,16]{2,1,0:T(8,128)} custom-call(bf16[2,256,1152]{2,1,0:T(8,128)(2,1)} %x_ref.1, f32[8,288]{1,0:T(8,128)} %pad_convert_fusion.act_ref, bf16[288,1728]{1,0:T(8,128)(2,1)} %ada_ref.1, bf16[288,2304]{1,0:T(8,128)(2,1)} %fada_ref.1, bf16[2,3,144,288]{3,2,1,0:T(8,128)(2,1)} %bitcast.21, bf16[2,144,288]{2,1,0:T(8,128)(2,1)} %bitcast.22, ...), custom_call_target="tpu_custom_call" | custom-call | tf_op jit(solution)/shard_map/dit_block/pallas_call | solution.py:488
  114.0 0.8 slice_select_fusion
  114.8 0.1 select_n.57
  114.9 0.1 select_n.59
  115.6 0.6 multiply_add_fusion
  (2 shorter events, 0.0 us)
Async XLA Ops:
  0.0 7.0 %copy-start.1 = (bf16[1152,16]{0,1:T(8,128)(2,1)S(1)}, bf16[1152,16]{0,1:T(8,128)(2,1)}, u32[]{:S(2)}) copy-start(bf16[1152,16]{0,1:T(8,128)(2,1)} %param.27) | copy-start | bytes 110596
  0.0 7.9 %copy-start = (bf16[288,288]{1,0:T(8,128)(2,1)S(1)}, bf16[288,288]{1,0:T(8,128)(2,1)}, u32[]{:S(2)}) copy-start(bf16[288,288]{1,0:T(8,128)(2,1)} %param.24) | copy-start | bytes 497668

commit v2 on v1

--- a/solution.py
+++ b/solution.py
@@ -182,16 +182,9 @@
 
 
 def copy_count(nd, nm):
-    per_weight = 2 * (nd - 1)
+    gather = 2 + 2 + nd
     return (
-        (nd - 1)
-        + (nd * nm - 1)
-        + (nm - 1)
-        + 3 * per_weight
-        + 2 * (nm - 1)
-        + per_weight
-        + 2 * (nm - 1)
-        + (nm - 1)
+        (nd - 1) + (nm - 1) + (nd * nm - 1) + (nm - 1) + 4 * gather + 4 * (nm - 1) + 2 * (nm - 1)
     )
 
 
@@ -215,11 +208,11 @@
     fmod_part,
     fmod_all,
     qkv_all,
+    proj_z,
     proj_all,
     fc1_all,
     fc2_all,
     h_ref,
-    q_ref,
     mix_all,
     x1_ref,
     gelu_ref,
@@ -230,7 +223,12 @@
 ):
     g, d, m = lax.axis_index("group"), lax.axis_index("dp"), lax.axis_index("mp")
     images, tokens, width = x_ref.shape
+    half = fc1_ref.shape[1]
+    low = (half + 31) // 32 * 16
+    parts = (pl.ds(0, low), pl.ds(low, half - low))
     sib = {"group": 1 - g}
+    near = (d + 1 - 2 * lax.rem(d, 2), lax.rem(d + 2, nd))
+    diag = nd - 1 - d
 
     def dpp(k):
         return lax.rem(d + k + nd, nd)
@@ -250,34 +248,50 @@
 
     cp = Copies(send_sem, recv_sem)
 
+    class Gather:
+        def __init__(self, buf, own_too=False):
+            self.buf, self.k, self.own_too = buf, cp.slots(2 + 2 + nd), own_too
+
+        def begin(self, src):
+            for n in range(2):
+                cp.start(src, self.buf.at[d, g], self.k + n, {"dp": near[n]})
+
+        def share(self, slot, n):
+            cp.start(self.buf.at[slot, g], self.buf.at[slot, g], self.k + 4 + n, sib)
+
+        def relay(self):
+            if self.own_too:
+                self.share(d, 0)
+            for n in range(2):
+                cp.arrived(self.buf.at[near[n], g], self.k + n, {"dp": near[n]})
+                piece = self.buf.at[near[n], g, parts[n]]
+                cp.start(piece, piece, self.k + 2 + n, {"dp": near[1 - n]})
+                self.share(near[n], 1 + n)
+
+        def last(self):
+            for n in range(2):
+                piece = self.buf.at[diag, g, parts[n]]
+                cp.arrived(piece, self.k + 2 + n, {"dp": near[1 - n]})
+            self.share(diag, 3)
+
+        def finish(self):
+            if self.own_too:
+                cp.arrived(self.buf.at[d, 1 - g], self.k + 4, sib)
+            for n, slot in enumerate((near[0], near[1], diag)):
+                cp.arrived(self.buf.at[slot, 1 - g], self.k + 5 + n, sib)
+
     k_act = cp.slots(nd - 1)
     for a in range(1, nd):
         cp.start(act_ref, act_all.at[d], k_act + a - 1, {"dp": dpp(a)})
+    qkv = Gather(qkv_all)
+    qkv.begin(qkv_ref.at[g])
     k_pz = cp.slots(nm - 1)
     for b in range(1, nm):
-        cp.start(proj_ref.at[g], proj_all.at[m, d, g], k_pz + b - 1, {"mp": mpp(b)})
-
-    def gather_start(src, buf):
-        k = cp.slots(nd - 1)
-        for a in range(1, nd):
-            cp.start(src.at[g], buf.at[d, g], k + a - 1, {"dp": dpp(a)})
-        return k
-
-    def gather_forward(buf, k):
-        kf = cp.slots(nd - 1)
-        for a in range(1, nd):
-            cp.arrived(buf.at[dpp(-a), g], k + a - 1, {"dp": dpp(-a)})
-            cp.start(buf.at[dpp(-a), g], buf.at[dpp(-a), g], kf + a - 1, sib)
-        return kf
-
-    def gather_finish(buf, kf):
-        for a in range(1, nd):
-            cp.arrived(buf.at[dpp(-a), 1 - g], kf + a - 1, sib)
-
-    k_qkv = gather_start(qkv_ref, qkv_all)
+        cp.start(proj_ref.at[g], proj_z.at[m], k_pz + b - 1, {"mp": mpp(b)})
+
     act_all[pl.ds(d, 1)] = act_ref[...][None]
     qkv_all[pl.ds(d, 1)] = qkv_ref[...][None]
-    proj_all[pl.ds(m, 1), pl.ds(d, 1)] = proj_ref[...][None, None]
+    proj_z[pl.ds(m, 1)] = proj_ref[pl.ds(g, 1)]
     fc1_all[pl.ds(d, 1)] = fc1_ref[...][None]
     fc2_all[pl.ds(d, 1)] = fc2_ref[...][None]
 
@@ -306,20 +320,15 @@
     for b in range(1, nm):
         cp.start(fmod_part, fmod_all.at[m], k_fmod + b - 1, {"mp": mpp(b)})
 
+    qkv.relay()
+    fc1 = Gather(fc1_all)
+    fc1.begin(fc1_ref.at[g])
+
     for b in range(1, nm):
-        cp.arrived(proj_all.at[mpp(-b), d, g], k_pz + b - 1, {"mp": mpp(-b)})
-    k_pd = cp.slots(nd - 1)
-    for a in range(1, nd):
-        cp.start(proj_all.at[:, d, g], proj_all.at[:, d, g], k_pd + a - 1, {"dp": dpp(a)})
-    k_fc1 = gather_start(fc1_ref, fc1_all)
-    k_fc2 = gather_start(fc2_ref, fc2_all)
-    f_qkv = gather_forward(qkv_all, k_qkv)
-    k_pzs = cp.slots(nm - 1)
-    for b in range(1, nm):
-        cp.start(
-            proj_all.at[mpp(-b), d, g], proj_all.at[mpp(-b), d, g], k_pzs + b - 1, sib
-        )
-
+        cp.arrived(proj_z.at[mpp(-b)], k_pz + b - 1, {"mp": mpp(-b)})
+    proj_all[pl.ds(d, 1), pl.ds(g, 1)] = jnp.concatenate(
+        [proj_z[b] for b in range(nm)], axis=1
+    )[None, None]
     for a in range(nd):
         for b in range(nm):
             if a or b:
@@ -346,64 +355,88 @@
             v = x_ref[i, rows, :].astype(F32)
             h_ref[i, rows, :] = (layer_norm(v) * (1.0 + scale) + shift).astype(BF)
 
-    gather_finish(qkv_all, f_qkv)
-    quarter = qkv_ref.shape[3]
+    qkv.last()
+    proj = Gather(proj_all, own_too=True)
+    proj.begin(proj_all.at[d, g])
+    qkv.finish()
+
+    quarter = qkv_ref.shape[2] // 3
     heads = quarter // head_dim
     lane = lax.broadcasted_iota(jnp.int32, (1, quarter), 1)
-    k_mix = cp.slots(images * (nm - 1))
+    k_mix = cp.slots(4 * (nm - 1))
+    fc2 = Gather(fc2_all)
+    held = []
+
+    def hop(i, h):
+        for way, sign in ((0, 1), (1, -1)):
+            k = k_mix + (way * 2 + i) * (nm - 1)
+            origin = m - sign * h
+            there = (m >= h) if way == 0 else (m < nm - h)
+            room = (m < nm - 1) if way == 0 else (m > 0)
+            block = mix_all.at[jnp.clip(origin, 0, nm - 1), i]
+            if h:
+
+                @pl.when(there)
+                def _():
+                    cp.make(block, block, k + h - 1, {"mp": mpp(-sign)}).wait_recv()
+
+            if h < nm - 1:
+                copy = cp.make(block, block, k + h, {"mp": mpp(sign)})
+                held.append((there & room, copy))
+
+                @pl.when(there & room)
+                def _():
+                    copy.start()
+
     for i in range(images):
-        for j in range(3):
-            w = qkv_all[:, :, j].reshape(width, quarter)
-            q_ref[j] = jnp.dot(h_ref[i], w, preferred_element_type=F32).astype(BF)
+        w = qkv_all[...].reshape(width, 3 * quarter)
+        mixed3 = jnp.dot(h_ref[i], w, preferred_element_type=F32).astype(BF)
+        query, key, value = (mixed3[:, j * quarter : (j + 1) * quarter] for j in range(3))
         total = jnp.zeros((tokens, quarter), F32)
         for n in range(heads):
             own = (lane >= n * head_dim) & (lane < (n + 1) * head_dim)
             own = jnp.where(own, 1.0, 0.0).astype(BF)
-            s = dot_nt(q_ref[0] * own, q_ref[1]) * head_dim ** (-0.5)
+            s = dot_nt(query * own, key) * head_dim ** (-0.5)
             e = jnp.exp(s - jnp.max(s, axis=-1, keepdims=True))
             p = (e / jnp.sum(e, axis=-1, keepdims=True)).astype(BF)
-            total = total + jnp.dot(p, q_ref[2] * own, preferred_element_type=F32)
-        mix_all[pl.ds(m, 1), i] = total.astype(BF)[None]
-        for b in range(1, nm):
-            cp.start(
-                mix_all.at[m, i],
-                mix_all.at[m, i],
-                k_mix + i * (nm - 1) + b - 1,
-                {"mp": mpp(b)},
-            )
-
-    k_pds = cp.slots(nd - 1)
-    for a in range(1, nd):
-        cp.arrived(proj_all.at[:, dpp(-a), g], k_pd + a - 1, {"dp": dpp(-a)})
-        cp.start(
-            proj_all.at[:, dpp(-a), g], proj_all.at[:, dpp(-a), g], k_pds + a - 1, sib
-        )
-    for b in range(1, nm):
-        cp.arrived(proj_all.at[mpp(-b), d, 1 - g], k_pzs + b - 1, sib)
-    f_fc1 = gather_forward(fc1_all, k_fc1)
-    for a in range(1, nd):
-        cp.arrived(proj_all.at[:, dpp(-a), 1 - g], k_pds + a - 1, sib)
-
+            total = total + jnp.dot(p, value * own, preferred_element_type=F32)
+        mix_all[pl.ds(m, 1), i] = total.T.astype(BF)[None]
+        hop(i, 0)
+        if i == 0:
+            fc1.relay()
+            fc2.begin(fc2_ref.at[g])
+
+    hop(0, 1)
+    proj.relay()
+    hop(1, 1)
+    fc1.last()
+    hop(0, 2)
+    hop(1, 2)
+    proj.last()
+    fc2.relay()
+    hop(0, 3)
+    proj.finish()
+
+    ff = fc1_ref.shape[2]
+    share = tokens // nm
+    k_rs = cp.slots(2 * (nm - 1))
     for i in range(images):
-        for b in range(1, nm):
-            cp.arrived(
-                mix_all.at[mpp(-b), i], k_mix + i * (nm - 1) + b - 1, {"mp": mpp(-b)}
-            )
+        if i:
+            hop(i, 3)
         gate, shift, scale = piece(2, i), piece(3, i), piece(4, i)
-
-        @pl.loop(0, 2)
+        full = mix_all[:, i].reshape(width, tokens).T
+        attn = dot_nt(full, proj_all[...].reshape(width, width))
+        x1_ref[i] = attn
+
+        @pl.loop(0, 4)
         def _(c):
-            rows = pl.ds(pl.multiple_of(c * 2 * step, 2 * step), 2 * step)
-            attn = jnp.zeros((2 * step, width), F32)
-            for b in range(nm):
-                attn = attn + dot_nt(mix_all[b, i, rows, :], proj_all[b].reshape(width, quarter))
-            v = x_ref[i, rows, :].astype(F32) + gate * attn
+            rows = pl.ds(pl.multiple_of(c * step, step), step)
+            v = x_ref[i, rows, :].astype(F32) + gate * x1_ref[i, rows, :]
             x1_ref[i, rows, :] = v
             h_ref[i, rows, :] = (layer_norm(v) * (1.0 + scale) + shift).astype(BF)
 
-    gather_finish(fc1_all, f_fc1)
-    ff = fc1_ref.shape[2]
-    for i in range(images):
+        if i == 0:
+            fc1.finish()
 
         @pl.loop(0, 2)
         def _(c):
@@ -413,34 +446,38 @@
             )
             gelu_ref[i, rows, :] = jax.nn.gelu(up, approximate=True).astype(BF)
 
-    f_fc2 = gather_forward(fc2_all, k_fc2)
-    gather_finish(fc2_all, f_fc2)
-
-    share = tokens // nm
-    k_rs = cp.slots(nm - 1)
+        if i == 0:
+            fc2.last()
+            fc2.finish()
+        rs_send[i] = dot_nt(gelu_ref[i], fc2_all[...].reshape(width, ff)).astype(BF)
+        for b in range(1, nm):
+            rows = pl.ds(pl.multiple_of(mpp(b) * share, share), share)
+            cp.start(
+                rs_send.at[i, rows],
+                rs_recv.at[i, b - 1],
+                k_rs + i * (nm - 1) + b - 1,
+                {"mp": mpp(b)},
+            )
+
     own_rows = pl.ds(pl.multiple_of(m * share, share), share)
-
-    def down(rows):
-        left = gelu_ref[:, rows, :].reshape(images * share, ff)
-        return dot_nt(left, fc2_all[...].reshape(width, ff))
-
-    for b in range(1, nm):
-        rows = pl.ds(pl.multiple_of(mpp(b) * share, share), share)
-        rs_send[b - 1] = down(rows).astype(BF)
-        cp.start(rs_send.at[b - 1], rs_recv.at[b - 1], k_rs + b - 1, {"mp": mpp(b)})
-    mlp = down(own_rows)
     for b in range(1, nm):
         cp.arrived(fmod_all.at[mpp(-b)], k_fmod + b - 1, {"mp": mpp(-b)})
     fmods = functools.reduce(jnp.add, [fmod_all[b] for b in range(nm)])
-    for b in range(1, nm):
-        cp.arrived(rs_recv.at[b - 1], k_rs + b - 1, {"mp": mpp(-b)})
-        mlp = mlp + rs_recv[b - 1].astype(F32)
     for i in range(images):
-        v = x1_ref[i, own_rows, :] + piece(5, i) * mlp[i * share : (i + 1) * share]
+        mlp = rs_send[i, own_rows, :].astype(F32)
+        for b in range(1, nm):
+            cp.arrived(rs_recv.at[i, b - 1], k_rs + i * (nm - 1) + b - 1, {"mp": mpp(-b)})
+            mlp = mlp + rs_recv[i, b - 1].astype(F32)
+        v = x1_ref[i, own_rows, :] + piece(5, i) * mlp
         shift, scale = fmods[i : i + 1, :width], fmods[i : i + 1, width:]
         fin = (layer_norm(v) * (1.0 + scale) + shift).astype(BF)
         eps_ref[i] = jnp.dot(fin, outw_ref[...], preferred_element_type=F32)
     cp.drain()
+    for cond, copy in held:
+
+        @pl.when(cond)
+        def _():
+            copy.wait_send()
 
 
 def on_device_kernel(
@@ -478,7 +515,7 @@
         )
     ).astype(BF)
     act = jnp.pad(act.astype(F32), ((0, 8 - images), (0, 0)))
-    qkv_in = qkv_weight.reshape(3, 2, half, quarter).transpose(1, 0, 2, 3)
+    qkv_in = qkv_weight.transpose(1, 0, 2).reshape(2, half, 3 * quarter)
     proj_in = proj_weight.T.reshape(2, half, quarter)
     fc1_in = fc1_weight.reshape(2, half, ff)
     fc2_in = fc2_weight.T.reshape(2, half, ff)
@@ -496,17 +533,17 @@
             pltpu.VMEM((nd, nm, images, ada_weight.shape[1]), F32),
             pltpu.VMEM((images, final_ada.shape[1]), F32),
             pltpu.VMEM((nm, images, final_ada.shape[1]), F32),
-            pltpu.VMEM((nd, 2, 3, half, quarter), BF),
-            pltpu.VMEM((nm, nd, 2, half, quarter), BF),
+            pltpu.VMEM((nd, 2, half, 3 * quarter), BF),
+            pltpu.VMEM((nm, half, quarter), BF),
+            pltpu.VMEM((nd, 2, half, width), BF),
             pltpu.VMEM((nd, 2, half, ff), BF),
             pltpu.VMEM((nd, 2, half, ff), BF),
             pltpu.VMEM((images, tokens, width), BF),
-            pltpu.VMEM((3, tokens, quarter), BF),
-            pltpu.VMEM((nm, images, tokens, quarter), BF),
+            pltpu.VMEM((nm, images, quarter, tokens), BF),
             pltpu.VMEM((images, tokens, width), F32),
             pltpu.VMEM((images, tokens, ff), BF),
-            pltpu.VMEM((nm - 1, images * share, width), BF),
-            pltpu.VMEM((nm - 1, images * share, width), BF),
+            pltpu.VMEM((images, tokens, width), BF),
+            pltpu.VMEM((images, nm - 1, share, width), BF),
             pltpu.SemaphoreType.DMA((copies,)),
             pltpu.SemaphoreType.DMA((copies,)),
         ],
@@ -550,6 +587,7 @@
     def body(*args):
         rows = args[9].shape[1]
         fits = args[0].shape[0] == 2 and mesh.shape["group"] == 2 and rows % 32 == 0
+        fits = fits and mesh.shape["dp"] == 4 and mesh.shape["mp"] == 4
         return on_device_kernel(*args) if fits else on_device(*args)
 
     return jax.shard_map(

time: 117 us -> 98.2 us (0.84)
  Pallas kernels: 105 us -> 85 us
    pallas_call x1, Pallas kernels: 105 us -> 85 us  [on_device_kernel(): pl.pallas_call(functools.partial(block_kernel, nd, nm, width // HEADS), o...]
    transpose x0 -> x1, local copies, waits for them, and re-layouts: none -> 1.59 us  [on_device_kernel(): qkv_in = qkv_weight.transpose(1, 0, 2).reshape(2, half, 3 * quarter)]
where the time goes in v2:
time: 98.2 us; the launch traced here: 96.8 us
  Pallas kernels  85 us (87%)
  local copies, waits for them, and re-layouts  5.95 us (6%)
  other arithmetic  3.1 us (3%)
  between operations  2.68 us (3%)
    pallas_call x1, Pallas kernels, on_device_kernel(): pl.pallas_call(functools.partial(block_kernel, nd, nm, width // HEADS), o...  85 us

profile of v2, /device:TPU:13, one launch (start us, length us, event | category | flops | bytes accessed | tf_op | source)
XLA Modules:
  0.0 96.8 jit_solution(7485715468656930199)
XLA Ops:
  0.7 1.0 %constant_dynamic-slice_fusion = (bf16[1,288]{0,1:T(8,128)(2,1)S(1)}, bf16[1,288]{0,1:T(8,128)(2,1)S(1)}) fusion(bf16[1001,288]{0,1:T(8,128)(2,1)} %param.20, s32[]{:T(128)S(6)} %select_n.53), kind=kLoop, calls=%fused_computation.10 | loop fusion | bytes 2308 | tf_op jit(solution)/shard_map/dynamic_slice | solution.py:505
  1.7 0.1 copy.25
  1.8 0.1 copy.26
  3.2 1.1 %convert_reduce_fusion = f32[288]{0:T(512)S(1)} fusion(bf16[1000,288]{0,1:T(8,128)(2,1)} %param.19, s32[]{:T(128)S(6)} %select_n.51), kind=kLoop, calls=%fused_computation | loop fusion | flops 288 | bytes 1732 | tf_op jit(solution)/shard_map/add | solution.py:509
  4.3 0.6 pad_convert_fusion.act_ref
  5.0 0.0 copy-start.1
  5.0 0.0 copy-start
  5.0 1.6 %copy.22 = bf16[288,3,288]{2,1,0:T(4,128)(2,1)S(1)} copy(bf16[288,3,288]{2,0,1:T(8,128)(2,1)} %bitcast.21) | data formatting | bytes 995328 | tf_op jit(solution)/shard_map/transpose | solution.py:518
  6.5 1.3 %reshape.60.qkv_ref = bf16[2,144,864]{2,1,0:T(8,128)(2,1)} reshape(bf16[288,3,288]{2,1,0:T(4,128)(2,1)S(1)} %copy.22) | data formatting | bytes 995328 | tf_op jit(solution)/shard_map/reshape | solution.py:518
  7.8 0.0 copy-done.1
  7.8 0.9 copy.24.outw_ref
  8.7 0.0 copy-done
  8.7 0.8 copy.23
  9.5 85.0 %dit_block.1 = f32[2,64,16]{2,1,0:T(8,128)} custom-call(bf16[2,256,1152]{2,1,0:T(8,128)(2,1)} %x_ref.1, f32[8,288]{1,0:T(8,128)} %pad_convert_fusion.act_ref, bf16[288,1728]{1,0:T(8,128)(2,1)} %ada_ref.1, bf16[288,2304]{1,0:T(8,128)(2,1)} %fada_ref.1, bf16[2,144,864]{2,1,0:T(8,128)(2,1)} %reshape.60.qkv_ref, bf16[2,144,288]{2,1,0:T(8,128)(2,1)} %bitcast.18, ...), custom_call_target="tpu_custom_call" | custom-call | tf_op jit(solution)/shard_map/dit_block/pallas_call | solution.py:525
  94.5 0.8 slice_select_fusion
  95.3 0.1 select_n.57
  95.4 0.1 select_n.59
  96.1 0.6 multiply_add_fusion
  (2 shorter events, 0.0 us)
Async XLA Ops:
  5.0 2.8 %copy-start.1 = (bf16[1152,16]{0,1:T(8,128)(2,1)S(1)}, bf16[1152,16]{0,1:T(8,128)(2,1)}, u32[]{:S(2)}) copy-start(bf16[1152,16]{0,1:T(8,128)(2,1)} %param.27) | copy-start | bytes 110596
  5.0 3.7 %copy-start = (bf16[288,288]{1,0:T(8,128)(2,1)S(1)}, bf16[288,288]{1,0:T(8,128)(2,1)}, u32[]{:S(2)}) copy-start(bf16[288,288]{1,0:T(8,128)(2,1)} %param.24) | copy-start | bytes 497668

commit v3 on v2

--- a/solution.py
+++ b/solution.py
@@ -208,6 +208,7 @@
     fmod_part,
     fmod_all,
     qkv_all,
+    proj_own,
     proj_z,
     proj_all,
     fc1_all,
@@ -236,6 +237,14 @@
     def mpp(k):
         return lax.rem(m + k + nm, nm)
 
+    quarter = qkv_ref.shape[2]
+    for n in range(2):
+        cut = slice(n * half, (n + 1) * half)
+        qkv_all[pl.ds(d, 1), n] = jnp.concatenate(
+            [qkv_ref[j, cut, :] for j in range(3)], axis=1
+        )[None]
+    proj_own[...] = proj_ref[...].astype(F32).T.astype(BF).reshape(proj_own.shape)
+
     barrier = pltpu.get_barrier_semaphore()
     for a in range(nd):
         for b in range(nm):
@@ -284,14 +293,13 @@
     for a in range(1, nd):
         cp.start(act_ref, act_all.at[d], k_act + a - 1, {"dp": dpp(a)})
     qkv = Gather(qkv_all)
-    qkv.begin(qkv_ref.at[g])
+    qkv.begin(qkv_all.at[d, g])
     k_pz = cp.slots(nm - 1)
     for b in range(1, nm):
-        cp.start(proj_ref.at[g], proj_z.at[m], k_pz + b - 1, {"mp": mpp(b)})
+        cp.start(proj_own.at[g], proj_z.at[m], k_pz + b - 1, {"mp": mpp(b)})
 
     act_all[pl.ds(d, 1)] = act_ref[...][None]
-    qkv_all[pl.ds(d, 1)] = qkv_ref[...][None]
-    proj_z[pl.ds(m, 1)] = proj_ref[pl.ds(g, 1)]
+    proj_z[pl.ds(m, 1)] = proj_own[pl.ds(g, 1)]
     fc1_all[pl.ds(d, 1)] = fc1_ref[...][None]
     fc2_all[pl.ds(d, 1)] = fc2_ref[...][None]
 
@@ -324,11 +332,6 @@
     fc1 = Gather(fc1_all)
     fc1.begin(fc1_ref.at[g])
 
-    for b in range(1, nm):
-        cp.arrived(proj_z.at[mpp(-b)], k_pz + b - 1, {"mp": mpp(-b)})
-    proj_all[pl.ds(d, 1), pl.ds(g, 1)] = jnp.concatenate(
-        [proj_z[b] for b in range(nm)], axis=1
-    )[None, None]
     for a in range(nd):
         for b in range(nm):
             if a or b:
@@ -356,11 +359,15 @@
             h_ref[i, rows, :] = (layer_norm(v) * (1.0 + scale) + shift).astype(BF)
 
     qkv.last()
+    for b in range(1, nm):
+        cp.arrived(proj_z.at[mpp(-b)], k_pz + b - 1, {"mp": mpp(-b)})
+    proj_all[pl.ds(d, 1), pl.ds(g, 1)] = jnp.concatenate(
+        [proj_z[b] for b in range(nm)], axis=1
+    )[None, None]
     proj = Gather(proj_all, own_too=True)
     proj.begin(proj_all.at[d, g])
     qkv.finish()
 
-    quarter = qkv_ref.shape[2] // 3
     heads = quarter // head_dim
     lane = lax.broadcasted_iota(jnp.int32, (1, quarter), 1)
     k_mix = cp.slots(4 * (nm - 1))
@@ -409,11 +416,11 @@
     hop(0, 1)
     proj.relay()
     hop(1, 1)
+    hop(0, 2)
     fc1.last()
-    hop(0, 2)
+    fc2.relay()
     hop(1, 2)
     proj.last()
-    fc2.relay()
     hop(0, 3)
     proj.finish()
 
@@ -471,7 +478,7 @@
         v = x1_ref[i, own_rows, :] + piece(5, i) * mlp
         shift, scale = fmods[i : i + 1, :width], fmods[i : i + 1, width:]
         fin = (layer_norm(v) * (1.0 + scale) + shift).astype(BF)
-        eps_ref[i] = jnp.dot(fin, outw_ref[...], preferred_element_type=F32)
+        eps_ref[i] = dot_nt(fin, outw_ref[...])
     cp.drain()
     for cond, copy in held:
 
@@ -515,8 +522,6 @@
         )
     ).astype(BF)
     act = jnp.pad(act.astype(F32), ((0, 8 - images), (0, 0)))
-    qkv_in = qkv_weight.transpose(1, 0, 2).reshape(2, half, 3 * quarter)
-    proj_in = proj_weight.T.reshape(2, half, quarter)
     fc1_in = fc1_weight.reshape(2, half, ff)
     fc2_in = fc2_weight.T.reshape(2, half, ff)
     copies = copy_count(nd, nm)
@@ -534,6 +539,7 @@
             pltpu.VMEM((images, final_ada.shape[1]), F32),
             pltpu.VMEM((nm, images, final_ada.shape[1]), F32),
             pltpu.VMEM((nd, 2, half, 3 * quarter), BF),
+            pltpu.VMEM((2, half, quarter), BF),
             pltpu.VMEM((nm, half, quarter), BF),
             pltpu.VMEM((nd, 2, half, width), BF),
             pltpu.VMEM((nd, 2, half, ff), BF),
@@ -556,11 +562,11 @@
         act,
         ada_weight,
         final_ada,
-        qkv_in,
-        proj_in,
+        qkv_weight,
+        proj_weight,
         fc1_in,
         fc2_in,
-        out_weight,
+        out_weight.T,
     )
     cond = jnp.where(first, eps[0], eps[1])
     uncond = jnp.where(first, eps[1], eps[0])

time: 98.2 us -> 93.8 us (0.955); the launches traced: 96.8 us -> 93.5 us
  local copies, waits for them, and re-layouts: 5.95 us -> 1.43 us
  Pallas kernels: 85 us -> 86.3 us
    transpose x2 -> x0, local copies, waits for them, and re-layouts: 2.42 us -> none  [the longest x1 1.59 us: on_device_kernel(): qkv_in = qkv_weight.transpose(1, 0, 2).reshape(2, half, 3 * quarter)]
    pallas_call x1, Pallas kernels: 85 us -> 86.3 us  [on_device_kernel(): pl.pallas_call(functools.partial(block_kernel, nd, nm, width // HEADS), o...]
    reshape x1 -> x0, local copies, waits for them, and re-layouts: 1.25 us -> none  [on_device_kernel(): qkv_in = qkv_weight.transpose(1, 0, 2).reshape(2, half, 3 * quarter)]
where the time goes in v3:
time: 93.8 us; the launch traced here: 93.5 us
  Pallas kernels  86.3 us (92%)
  other arithmetic  3.1 us (3%)
  between operations  2.68 us (3%)
  local copies, waits for them, and re-layouts  1.43 us (2%)
    pallas_call x1, Pallas kernels, on_device_kernel(): pl.pallas_call(functools.partial(block_kernel, nd, nm, width // HEADS), o...  86.3 us

profile of v3, /device:TPU:13, one launch (start us, length us, event | category | flops | bytes accessed | tf_op | source)
XLA Modules:
  0.0 93.5 jit_solution(15741938877903176397)
XLA Ops:
  0.7 1.1 %constant_dynamic-slice_fusion = (bf16[1,288]{0,1:T(8,128)(2,1)S(1)}, bf16[1,288]{0,1:T(8,128)(2,1)S(1)}) fusion(bf16[1001,288]{0,1:T(8,128)(2,1)} %param.20, s32[]{:T(128)S(6)} %select_n.53), kind=kLoop, calls=%fused_computation.10 | loop fusion | bytes 2308 | tf_op jit(solution)/shard_map/dynamic_slice | solution.py:512
  1.7 0.1 copy.19
  1.8 0.1 copy.20
  3.3 1.1 %convert_reduce_fusion = f32[288]{0:T(512)S(1)} fusion(bf16[1000,288]{0,1:T(8,128)(2,1)} %param.19, s32[]{:T(128)S(6)} %select_n.51), kind=kLoop, calls=%fused_computation | loop fusion | flops 288 | bytes 1732 | tf_op jit(solution)/shard_map/add | solution.py:516
  4.4 0.6 pad_convert_fusion.act_ref
  5.0 86.3 %dit_block.1 = f32[2,64,16]{2,1,0:T(8,128)} custom-call(bf16[2,256,1152]{2,1,0:T(8,128)(2,1)} %x_ref.1, f32[8,288]{1,0:T(8,128)} %pad_convert_fusion.act_ref, bf16[288,1728]{1,0:T(8,128)(2,1)} %ada_ref.1, bf16[288,2304]{1,0:T(8,128)(2,1)} %fada_ref.1, bf16[3,288,288]{2,1,0:T(8,128)(2,1)} %qkv_ref.1, bf16[288,288]{1,0:T(8,128)(2,1)} %proj_ref.1, ...), custom_call_target="tpu_custom_call" | custom-call | tf_op jit(solution)/shard_map/dit_block/pallas_call | solution.py:530
  91.3 0.8 slice_select_fusion
  92.1 0.1 select_n.57
  92.2 0.1 select_n.59
  92.9 0.6 multiply_add_fusion
  (2 shorter events, 0.0 us)
